TPU v7x, 32 devices: a 4x4x1 block of a 4x4x8 slice. The times are simulated.
32 devices in a mesh: dp: 2 (over z, core), sp: 16 (over x, y).
Axes of the slice: x: 4, y: 4, z: 1, core: 2. Of those that a mesh axis runs over, the one named last changes fastest.
The devices are a block of a 4x4x8 slice.
Arguments:
- q: bfloat16 [64, 32, 96], P('dp'), parts along dimension 0
- k: bfloat16 [64, 4096, 32, 96], P('dp', 'sp'), parts along dimension 0
- v: bfloat16 [64, 4096, 32, 96], P('dp', 'sp'), parts along dimension 0
Outputs:
- q: bfloat16 [64, 32, 96], P('dp'), parts along dimension 0
There are 2 independent parts. A program takes and returns all parts, laid end to end along the dimension named above; each array names one.
All inputs are finite; a program needn't handle non-finite values.
Results may differ from a plain program's by a relative error of at most 0.012.
Values are sent between devices in bfloat16 or wider.
A program may use at most 768 MiB of HBM per device.

v0:
```python
import jax
import jax.numpy as jnp
from jax import lax
from jax.sharding import PartitionSpec as P


def einsum(form, a, b):
    return jnp.einsum(form, a.astype(jnp.float32), b.astype(jnp.float32))


def part_of(q, k, v):
    grouped = q.reshape(q.shape[0], k.shape[2], -1, q.shape[2])
    scores = einsum("bgsd,bugd->bgsu", grouped, k) * q.shape[2] ** -0.5
    high = jnp.max(scores, -1, keepdims=True)
    weights = jnp.exp(scores - high)
    seen = einsum("bgsu,bugd->bgsd", weights.astype(jnp.bfloat16), v)
    return jnp.concatenate([seen, jnp.sum(weights, -1, keepdims=True), high], -1)


def together(parts):
    seen, total, high = parts[..., :-2], parts[..., -2:-1], parts[..., -1:]
    scale = jnp.exp(high - jnp.max(high, 0))
    return (jnp.sum(seen * scale, 0) / jnp.sum(total * scale, 0)).astype(jnp.bfloat16)


def solution(mesh):
    def step(q, k, v):
        return together(lax.all_gather(part_of(q, k, v), "sp")).reshape(q.shape)

    return jax.shard_map(
        step,
        mesh=mesh,
        in_specs=(P("dp", None, None), P("dp", "sp", None, None), P("dp", "sp", None, None)),
        out_specs=P("dp", None, None),
        check_vma=False,
    )
```

profile of v0, /device:TPU:97, one launch (start us, length us, event | category | flops | bytes accessed | tf_op | source)
XLA Modules:
  0.0 153.6 jit_solution(8066818012202787010)
XLA Ops:
  6.5 0.0 all-gather.3.cloned.1.call-start
  6.6 18.0 %fusion.7 = f32[32,32,1,256]{3,2,1,0:T(1,128)S(1)} fusion(bf16[32,256,32,96]{1,3,2,0:T(8,128)(2,1)} %param.4, bf16[32,32,96,1]{2,1,0,3:T(8,128)(2,1)} %bitcast.27), kind=kOutput, calls=%fused_computation.12 | convolution fusion | flops 50331648 | bytes 51576832 | tf_op jit(solution)/shard_map/bgsd,bugd->bgsu/dot_general | solution.py:8
  24.6 0.2 fusion.5
  24.8 0.4 fusion.6
  25.2 0.3 copy.17
  25.5 0.3 copy.16
  25.8 19.7 %fusion.1 = f32[32,32,1,96]{3,2,1,0:T(1,128)S(1)} fusion(bf16[32,256,32,96]{1,3,2,0:T(8,128)(2,1)} %param.5, bf16[32,32,256,1]{2,1,0,3:T(8,128)(2,1)S(1)} %get-tuple-element.7), kind=kOutput, calls=%fused_computation.4 | convolution fusion | flops 50331648 | bytes 51249152 | tf_op jit(solution)/shard_map/bgsu,bugd->bgsd/dot_general | solution.py:8
  45.4 1.1 pad_maximum_fusion
  46.6 0.1 all-gather.3.cloned.1.call-update
  46.6 69.3 %all-gather.3.cloned.1.call-done = f32[512,32,1,98]{3,1,2,0:T(8,128)} async-done(((f32[32,32,1,98]{3,1,2,0:T(8,128)}), f32[512,32,1,98]{3,1,2,0:T(8,128)}) %all-gather.3.cloned.1.call-update) | async-done | bytes 6422544 | tf_op jit(solution)/shard_map/all_gather | solution.py:28
  115.9 17.0 %copy.18 = f32[512,32,1,98]{1,0,3,2:T(8,128)} copy(f32[512,32,1,98]{3,1,2,0:T(8,128)} %all-gather.3.cloned.1.call-done) | data formatting | bytes 12845056 | tf_op jit(solution)/shard_map/all_gather | solution.py:28
  132.9 1.0 slice_reduce_fusion
  133.9 1.1 fusion.9
  135.0 10.0 %fusion = f32[32,32,96]{1,0,2:T(8,128)S(1)} fusion(f32[16,32,32,1,98]{2,1,0,4,3:T(8,128)} %bitcast.25, f32[16,32,32]{2,1,0:T(8,128)S(1)} %get-tuple-element.6), kind=kLoop, calls=%fused_computation.1 | loop fusion | flops 3047424 | bytes 6750208 | tf_op jit(solution)/shard_map/reduce_sum | solution.py:23
  145.0 0.2 divide_convert_fusion
  145.2 1.5 copy.19
Async XLA Ops:
  6.5 109.4 %all-gather.3.cloned.1.call-start = ((), (), s32[]{:S(2)}) async-start(), calls=%async_computation | async-start | bytes 8912896 | tf_op jit(solution)/shard_map/all_gather | solution.py:28
Sparse Core Ops, SparseCore 0:
  46.8 69.1 all-gather.2
where the time goes:
time: 154 us
  waiting for transfers between devices  69.3 us (45%)
  matrix products  37.7 us (24%)
  local copies, waits for them, and re-layouts  19.1 us (12%)
  other arithmetic  14.1 us (9%)
  between operations  13.5 us (9%)
    all_gather x1, waiting for transfers between devices, step(): return together(lax.all_gather(part_of(q, k, v), 'sp')).reshape(q.shape)  69.3 us
    dot_general x2, matrix products, einsum(): return jnp.einsum(form, a.astype(jnp.float32), b.astype(jnp.float32))  37.7 us
    all_gather x1, local copies, waits for them, and re-layouts, step(): return together(lax.all_gather(part_of(q, k, v), 'sp')).reshape(q.shape)  17 us
    reduce_sum x1, other arithmetic, together(): jnp.sum(seen * scale, 0) / jnp.sum(total * scale, 0)  10 us
  transfers between devices with their start and end apart: 1, of which 1 were waited for; matrix products, arithmetic and copies ran while one was open for 0% of the time, Pallas kernels for 0%

commit v1 on v0

v1 whole, which is shorter than its diff:
```python
import functools
import math

import jax
import jax.numpy as jnp
from jax import lax
from jax.experimental import pallas as pl
from jax.experimental.pallas import tpu as pltpu
from jax.sharding import PartitionSpec as P

MESH = pl.DeviceIdType.MESH
LANES = 128
ROWS = 8
TURN = 16
SLOTS = 4


def kernel(n, q_hbm, k_hbm, v_hbm, out_ref, q_raw, q_wide, keys, values, parts, others, done, q_sem, k_sem, v_sem, send_sem, recv_sem, out_send, out_recv, own_sem):
    batch, heads, head = q_hbm.shape
    tokens = k_hbm.shape[1]
    own = batch // n
    unit = own * heads * head
    span = ROWS * head
    me = lax.axis_index("sp")
    side = math.isqrt(n)

    def peer(step):
        if side * side != n:
            return lax.rem(me + step, n)
        x = lax.rem(me // side + step // side, side)
        y = lax.rem(lax.rem(me, side) + lax.rem(step, side), side)
        return x * side + y

    def fetch(j, slot):
        rows = pl.ds(pl.multiple_of(peer(n - 1 - j) * unit, unit), unit)
        return (
            pltpu.make_async_copy(k_hbm.at[rows], keys.at[slot], k_sem.at[slot]),
            pltpu.make_async_copy(v_hbm.at[rows], values.at[slot], v_sem.at[slot]),
        )

    q_copy = pltpu.make_async_copy(q_hbm, q_raw, q_sem)
    q_copy.start()
    for j in range(min(SLOTS, n)):
        for copy in fetch(j, j):
            copy.start()

    barrier = pltpu.get_barrier_semaphore()

    def greet(step, _):
        pl.semaphore_signal(barrier, inc=1, device_id={"sp": peer(step)}, device_id_type=MESH)
        return 0

    lax.fori_loop(1, n, greet, 0)
    q_copy.wait()
    q_wide[:, :, :head] = q_raw[...].astype(jnp.float32)
    plain = q_wide[...].reshape(batch * heads, LANES)
    turned = plain
    for row in range(1, LANES // math.gcd(head, LANES)):
        take = lax.rem(lax.broadcasted_iota(jnp.int32, plain.shape, 0), LANES // math.gcd(head, LANES)) == row
        turned = jnp.where(take, pltpu.roll(plain, row * head % LANES, 1), turned)
    q_wide[...] = turned.reshape(batch, heads, LANES)
    pl.semaphore_wait(barrier, n - 1)

    row = lax.broadcasted_iota(jnp.int32, (ROWS, LANES), 0)
    lane = lax.broadcasted_iota(jnp.int32, (ROWS, LANES), 1)
    inside = []
    for block in range(span // LANES):
        at = lane + block * LANES - row * head
        inside.append((at >= 0) & (at < head))

    def attend(step, slot):
        first = peer(step) * own
        for s in range(own):
            for g in range(heads // ROWS):
                base = (s * heads + g * ROWS) * head
                query = q_wide[first + s, pl.ds(g * ROWS, ROWS), :]
                query = jnp.concatenate([jnp.where(i, query, 0.0) for i in inside], 1).astype(jnp.bfloat16)
                scores = jnp.dot(query, keys[slot, pl.ds(base, span), :], preferred_element_type=jnp.float32)
                scores = scores * head**-0.5
                high = jnp.max(scores, -1, keepdims=True)
                weights = jnp.exp(scores - high)
                total = jnp.sum(weights, -1, keepdims=True)
                seen = lax.dot_general(
                    weights.astype(jnp.bfloat16),
                    values[slot, pl.ds(base, span), :],
                    (((1,), (1,)), ((), ())),
                    preferred_element_type=jnp.float32,
                )
                mine = seen[:, :LANES]
                for block in range(1, span // LANES):
                    mine = jnp.where(inside[block], seen[:, block * LANES : (block + 1) * LANES], mine)
                for _ in range((LANES - head) // TURN):
                    mine = pltpu.roll(mine, 0, 1, stride=TURN, stride_axis=0)
                mine = jnp.where(lane < head, mine, jnp.where(lane == head, total, high))
                parts[step, pl.ds(s * heads + g * ROWS, ROWS), :] = mine

    def send(step):
        return pltpu.make_async_remote_copy(
            src_ref=parts.at[step],
            dst_ref=others.at[step],
            send_sem=send_sem.at[step],
            recv_sem=recv_sem.at[step],
            device_id={"sp": peer(step)},
            device_id_type=MESH,
        )

    def work(j, _):
        slot = lax.rem(j, SLOTS)
        for copy in fetch(j, slot):
            copy.wait()
        attend(n - 1 - j, slot)
        send(n - 1 - j).start()

        @pl.when(j + SLOTS < n)
        def _():
            for copy in fetch(j + SLOTS, slot):
                copy.start()

        return 0

    lax.fori_loop(0, n - 1, work, 0)
    last = (n - 1) % SLOTS
    for copy in fetch(n - 1, last):
        copy.wait()
    attend(0, last)

    for step in range(1, n):
        send(step).wait_recv()
    runs = [parts[0]] + [others[step] for step in range(1, n)]
    top = functools.reduce(jnp.maximum, [run[:, head + 1 : head + 2] for run in runs])
    sums = sum(run * jnp.exp(run[:, head + 1 : head + 2] - top) for run in runs)
    result = sums[:, :head] / sums[:, head : head + 1]
    done[...] = result.astype(jnp.bfloat16).reshape(done.shape)

    mine = pl.ds(me * own, own)
    keep = pltpu.make_async_copy(done, out_ref.at[mine], own_sem)
    keep.start()

    def give(step):
        return pltpu.make_async_remote_copy(
            src_ref=done,
            dst_ref=out_ref.at[mine],
            send_sem=out_send.at[step],
            recv_sem=out_recv.at[step],
            device_id={"sp": peer(step)},
            device_id_type=MESH,
        )

    for step in reversed(range(1, n)):
        give(step).start()
    for step in range(1, n):
        send(step).wait_send()
    for step in range(1, n):
        give(step).wait()
    keep.wait()


def solution(mesh):
    n = mesh.shape["sp"]

    def step(q, k, v):
        batch, tokens, heads, head = k.shape
        own = batch // n
        rows = own * heads
        unit = rows * head
        flat = lambda x: x.transpose(0, 2, 3, 1).reshape(batch * heads * head, tokens)
        return pl.pallas_call(
            functools.partial(kernel, n),
            out_shape=jax.ShapeDtypeStruct(q.shape, jnp.bfloat16),
            in_specs=[pl.BlockSpec(memory_space=pl.ANY)] * 3,
            out_specs=pl.BlockSpec(memory_space=pl.ANY),
            scratch_shapes=[
                pltpu.VMEM(q.shape, jnp.bfloat16),
                pltpu.VMEM((batch, heads, LANES), jnp.float32),
                pltpu.VMEM((SLOTS, unit, tokens), jnp.bfloat16),
                pltpu.VMEM((SLOTS, unit, tokens), jnp.bfloat16),
                pltpu.VMEM((n, rows, LANES), jnp.float32),
                pltpu.VMEM((n, rows, LANES), jnp.float32),
                pltpu.VMEM((own, heads, head), jnp.bfloat16),
                pltpu.SemaphoreType.DMA,
                pltpu.SemaphoreType.DMA((SLOTS,)),
                pltpu.SemaphoreType.DMA((SLOTS,)),
                pltpu.SemaphoreType.DMA((n,)),
                pltpu.SemaphoreType.DMA((n,)),
                pltpu.SemaphoreType.DMA((n,)),
                pltpu.SemaphoreType.DMA((n,)),
                pltpu.SemaphoreType.DMA,
            ],
            compiler_params=pltpu.CompilerParams(collective_id=0, has_side_effects=True, vmem_limit_bytes=60 * 2**20),
        )(q, flat(k), flat(v))

    return jax.shard_map(
        step,
        mesh=mesh,
        in_specs=(P("dp", None, None), P("dp", "sp", None, None), P("dp", "sp", None, None)),
        out_specs=P("dp", None, None),
        check_vma=False,
    )
```

time: 154 us -> 73 us (0.47)
  Pallas kernels: 0 us -> 71.2 us
  waiting for transfers between devices: 69.3 us -> 0 us
  matrix products: 37.7 us -> 0 us
  local copies, waits for them, and re-layouts: 19.1 us -> 1.67 us
  other arithmetic: 14.1 us -> 0 us
  between operations: 13.5 us -> 0.01 us
    pallas_call x0 -> x1, Pallas kernels: none -> 71.2 us  [step(): pl.pallas_call(functools.partial(kernel, n), out_shape=jax.ShapeDtypeStru...]
    all_gather x1 -> x0, waiting for transfers between devices: 69.3 us -> none  [step(): return together(lax.all_gather(part_of(q, k, v), 'sp')).reshape(q.shape)]
    dot_general x2 -> x0, matrix products: 37.7 us -> none  [einsum(): return jnp.einsum(form, a.astype(jnp.float32), b.astype(jnp.float32))]
    all_gather x1 -> x0, local copies, waits for them, and re-layouts: 17 us -> none  [step(): return together(lax.all_gather(part_of(q, k, v), 'sp')).reshape(q.shape)]
    reduce_sum x2 -> x0, other arithmetic: 11.1 us -> none  [the longest x1 10 us: together(): jnp.sum(seen * scale, 0) / jnp.sum(total * scale, 0)]
    unnamed x0 -> x1, local copies, waits for them, and re-layouts: none -> 1.67 us
  transfers between devices with their start and end apart: 1 -> 0, of which waited for: 1 -> 0; matrix products, arithmetic and copies ran while one was open for 0% -> 0% of each run, Pallas kernels for 0% -> 0%
where the time goes in v1:
time: 73 us; the launch traced here: 72.9 us
  Pallas kernels  71.2 us (98%)
  local copies, waits for them, and re-layouts  1.67 us (2%)
    pallas_call x1, Pallas kernels, step(): pl.pallas_call(functools.partial(kernel, n), out_shape=jax.ShapeDtypeStru...  71.2 us
    unnamed x1, local copies, waits for them, and re-layouts  1.67 us

profile of v1, /device:TPU:97, one launch (start us, length us, event | category | flops | bytes accessed | tf_op | source)
XLA Modules:
  0.0 72.9 jit_solution(8707278027896432785)
XLA Ops:
  0.0 71.2 %shard_map.37 = bf16[32,32,96]{2,1,0:T(8,128)(2,1)} custom-call(bf16[32,32,96]{2,1,0:T(8,128)(2,1)} %q_hbm.1, bf16[98304,256]{1,0:T(8,128)(2,1)} %bitcast.6, bf16[98304,256]{1,0:T(8,128)(2,1)} %bitcast.7), custom_call_target="tpu_custom_call" | custom-call | tf_op jit(solution)/shard_map/pallas_call | solution.py:167
  71.2 1.7 %copy.5 = bf16[32,32,96]{2,1,0:T(8,128)(2,1)} copy(bf16[32,32,96]{2,1,0:T(8,128)(2,1)} %shard_map.37) | data formatting | bytes 393216

commit v2 on v1

--- a/solution.py
+++ b/solution.py
@@ -11,16 +11,18 @@
 MESH = pl.DeviceIdType.MESH
 LANES = 128
 ROWS = 8
+CHUNK = 8
 TURN = 16
 SLOTS = 4
 
 
-def kernel(n, q_hbm, k_hbm, v_hbm, out_ref, q_raw, q_wide, keys, values, parts, others, done, q_sem, k_sem, v_sem, send_sem, recv_sem, out_send, out_recv, own_sem):
+def kernel(n, q_hbm, k_hbm, v_hbm, out_ref, q_raw, q_wide, keys, values, scores, parts, others, done, q_sem, k_sem, v_sem, send_sem, recv_sem, out_send, out_recv, own_sem):
     batch, heads, head = q_hbm.shape
     tokens = k_hbm.shape[1]
     own = batch // n
     unit = own * heads * head
     span = ROWS * head
+    count = own * heads
     me = lax.axis_index("sp")
     side = math.isqrt(n)
 
@@ -31,18 +33,15 @@
         y = lax.rem(lax.rem(me, side) + lax.rem(step, side), side)
         return x * side + y
 
-    def fetch(j, slot):
+    def fetch(source, target, sem, j, slot):
         rows = pl.ds(pl.multiple_of(peer(n - 1 - j) * unit, unit), unit)
-        return (
-            pltpu.make_async_copy(k_hbm.at[rows], keys.at[slot], k_sem.at[slot]),
-            pltpu.make_async_copy(v_hbm.at[rows], values.at[slot], v_sem.at[slot]),
-        )
+        return pltpu.make_async_copy(source.at[rows], target.at[slot], sem.at[slot])
 
     q_copy = pltpu.make_async_copy(q_hbm, q_raw, q_sem)
     q_copy.start()
     for j in range(min(SLOTS, n)):
-        for copy in fetch(j, j):
-            copy.start()
+        fetch(k_hbm, keys, k_sem, j, j).start()
+        fetch(v_hbm, values, v_sem, j, j).start()
 
     barrier = pltpu.get_barrier_semaphore()
 
@@ -62,27 +61,34 @@
     pl.semaphore_wait(barrier, n - 1)
 
     row = lax.broadcasted_iota(jnp.int32, (ROWS, LANES), 0)
-    lane = lax.broadcasted_iota(jnp.int32, (ROWS, LANES), 1)
+    lane = lax.broadcasted_iota(jnp.int32, (count, LANES), 1)
+    column = lax.broadcasted_iota(jnp.int32, (head, count), 1)
     inside = []
     for block in range(span // LANES):
-        at = lane + block * LANES - row * head
+        at = lane[:ROWS] + block * LANES - row * head
         inside.append((at >= 0) & (at < head))
 
-    def attend(step, slot):
+    def score(step, slot, groups):
         first = peer(step) * own
-        for s in range(own):
-            for g in range(heads // ROWS):
-                base = (s * heads + g * ROWS) * head
-                query = q_wide[first + s, pl.ds(g * ROWS, ROWS), :]
-                query = jnp.concatenate([jnp.where(i, query, 0.0) for i in inside], 1).astype(jnp.bfloat16)
-                scores = jnp.dot(query, keys[slot, pl.ds(base, span), :], preferred_element_type=jnp.float32)
-                scores = scores * head**-0.5
-                high = jnp.max(scores, -1, keepdims=True)
-                weights = jnp.exp(scores - high)
-                total = jnp.sum(weights, -1, keepdims=True)
+        for g in groups:
+            query = q_wide[first + g * ROWS // heads, pl.ds(g * ROWS % heads, ROWS), :]
+            query = jnp.concatenate([jnp.where(i, query, 0.0) for i in inside], 1).astype(jnp.bfloat16)
+            scores[g * ROWS : (g + 1) * ROWS, :] = jnp.dot(
+                query, keys[slot, pl.ds(g * span, span), :], preferred_element_type=jnp.float32
+            ) * head**-0.5
+
+    def attend(step, slot, after):
+        drawn = scores[...]
+        high = jnp.max(drawn, -1, keepdims=True)
+        weights = jnp.exp(drawn - high)
+        total = jnp.sum(weights, -1, keepdims=True)
+        for c in range(count // CHUNK):
+            after(c)
+            for g in range(c * CHUNK // ROWS, (c + 1) * CHUNK // ROWS):
+                at = slice(g * ROWS, (g + 1) * ROWS)
                 seen = lax.dot_general(
-                    weights.astype(jnp.bfloat16),
-                    values[slot, pl.ds(base, span), :],
+                    weights[at].astype(jnp.bfloat16),
+                    values[slot, pl.ds(g * span, span), :],
                     (((1,), (1,)), ((), ())),
                     preferred_element_type=jnp.float32,
                 )
@@ -91,8 +97,7 @@
                     mine = jnp.where(inside[block], seen[:, block * LANES : (block + 1) * LANES], mine)
                 for _ in range((LANES - head) // TURN):
                     mine = pltpu.roll(mine, 0, 1, stride=TURN, stride_axis=0)
-                mine = jnp.where(lane < head, mine, jnp.where(lane == head, total, high))
-                parts[step, pl.ds(s * heads + g * ROWS, ROWS), :] = mine
+                parts[step, at, :] = jnp.where(lane[:ROWS] < head, mine, jnp.where(lane[:ROWS] == head, total[at], high[at]))
 
     def send(step):
         return pltpu.make_async_remote_copy(
@@ -104,25 +109,40 @@
             device_id_type=MESH,
         )
 
+    def nothing(c):
+        pass
+
     def work(j, _):
-        slot = lax.rem(j, SLOTS)
-        for copy in fetch(j, slot):
-            copy.wait()
-        attend(n - 1 - j, slot)
+        slot, later = lax.rem(j, SLOTS), lax.rem(j + 1, SLOTS)
+        fetch(k_hbm, keys, k_sem, j + 1, later).wait()
+        fetch(v_hbm, values, v_sem, j, slot).wait()
+        groups = count // ROWS
+        chunks = count // CHUNK
+
+        def ahead(c):
+            score(n - 2 - j, later, range(c * groups // chunks, (c + 1) * groups // chunks))
+
+        attend(n - 1 - j, slot, ahead)
         send(n - 1 - j).start()
+
+        @pl.when(j + 1 + SLOTS < n)
+        def _():
+            fetch(k_hbm, keys, k_sem, j + 1 + SLOTS, later).start()
 
         @pl.when(j + SLOTS < n)
         def _():
-            for copy in fetch(j + SLOTS, slot):
-                copy.start()
+            fetch(v_hbm, values, v_sem, j + SLOTS, slot).start()
 
         return 0
 
+    fetch(k_hbm, keys, k_sem, 0, 0).wait()
+    score(n - 1, 0, range(count // ROWS))
+    if SLOTS < n:
+        fetch(k_hbm, keys, k_sem, SLOTS, 0).start()
     lax.fori_loop(0, n - 1, work, 0)
     last = (n - 1) % SLOTS
-    for copy in fetch(n - 1, last):
-        copy.wait()
-    attend(0, last)
+    fetch(v_hbm, values, v_sem, n - 1, last).wait()
+    attend(0, last, nothing)
 
     for step in range(1, n):
         send(step).wait_recv()
@@ -174,6 +194,7 @@
                 pltpu.VMEM((batch, heads, LANES), jnp.float32),
                 pltpu.VMEM((SLOTS, unit, tokens), jnp.bfloat16),
                 pltpu.VMEM((SLOTS, unit, tokens), jnp.bfloat16),
+                pltpu.VMEM((rows, tokens), jnp.float32),
                 pltpu.VMEM((n, rows, LANES), jnp.float32),
                 pltpu.VMEM((n, rows, LANES), jnp.float32),
                 pltpu.VMEM((own, heads, head), jnp.bfloat16),

time: 73 us -> 46.9 us (0.64)
  Pallas kernels: 71.2 us -> 45.1 us
    pallas_call x1, Pallas kernels: 71.2 us -> 45.1 us  [step(): pl.pallas_call(functools.partial(kernel, n), out_shape=jax.ShapeDtypeStru...]
where the time goes in v2:
time: 46.9 us; the launch traced here: 46.8 us
  Pallas kernels  45.1 us (96%)
  local copies, waits for them, and re-layouts  1.67 us (4%)
    pallas_call x1, Pallas kernels, step(): pl.pallas_call(functools.partial(kernel, n), out_shape=jax.ShapeDtypeStru...  45.1 us
    unnamed x1, local copies, waits for them, and re-layouts  1.67 us

profile of v2, /device:TPU:97, one launch (start us, length us, event | category | flops | bytes accessed | tf_op | source)
XLA Modules:
  0.0 46.8 jit_solution(3589974464199055982)
XLA Ops:
  0.0 45.1 %shard_map.37 = bf16[32,32,96]{2,1,0:T(8,128)(2,1)} custom-call(bf16[32,32,96]{2,1,0:T(8,128)(2,1)} %q_hbm.1, bf16[98304,256]{1,0:T(8,128)(2,1)} %bitcast.6, bf16[98304,256]{1,0:T(8,128)(2,1)} %bitcast.7), custom_call_target="tpu_custom_call" | custom-call | tf_op jit(solution)/shard_map/pallas_call | solution.py:187
  45.1 1.7 %copy.5 = bf16[32,32,96]{2,1,0:T(8,128)(2,1)} copy(bf16[32,32,96]{2,1,0:T(8,128)(2,1)} %shard_map.37) | data formatting | bytes 393216

commit v3 on v0

v3 whole, which is shorter than its diff:
```python
import functools
import math

import jax
import jax.numpy as jnp
from jax import lax
from jax.experimental import pallas as pl
from jax.experimental.pallas import tpu as pltpu
from jax.sharding import PartitionSpec as P

MESH = pl.DeviceIdType.MESH
LANES = 128
ROWS = 8
TURN = 16
PHASES = 2
LATE = 4
SLOTS = 4


def kernel(
    n, q_hbm, k_hbm, v_hbm, out_ref, q_raw, q_wide, keys, values, weights, seen, parts, others, done, q_sem, k_sem, v_sem, send_sem, recv_sem, out_send, out_recv, own_sem
):
    batch, heads, head = q_hbm.shape
    own = batch // n
    some = heads // PHASES
    count = own * some
    groups = some // ROWS
    span = ROWS * head
    units = PHASES * (n - 1)
    me = lax.axis_index("sp")

    def peer(step):
        if n & (n - 1) == 0:
            return me ^ step
        return lax.rem(me + step, n)

    def where(j):
        if isinstance(j, int):
            return (j // (n - 1), n - 1 - j % (n - 1)) if j < units else (j - units, 0)
        phase = sum((j >= (n - 1) * p).astype(jnp.int32) for p in range(1, PHASES)) if PHASES > 1 else 0
        theirs = j < units
        return jnp.where(theirs, phase, j - units), jnp.where(theirs, n - 1 - j + phase * (n - 1), 0)

    def fetch(source, target, sem, j):
        phase, step = where(j)
        slot = j & (SLOTS - 1)
        rows = pl.ds(phase * (some * head), some * head)
        return pltpu.make_async_copy(source.at[pl.ds(peer(step) * own, own), rows], target.at[slot], sem.at[slot])

    fetch_k = functools.partial(fetch, k_hbm, keys, k_sem)
    fetch_v = functools.partial(fetch, v_hbm, values, v_sem)

    q_copy = pltpu.make_async_copy(q_hbm, q_raw, q_sem)
    q_copy.start()
    for j in range(SLOTS):
        fetch_k(j).start()
        fetch_v(j).start()

    barrier = pltpu.get_barrier_semaphore()

    def greet(step, _):
        pl.semaphore_signal(barrier, inc=1, device_id={"sp": peer(step)}, device_id_type=MESH)
        return 0

    lax.fori_loop(1, n, greet, 0)
    q_copy.wait()
    q_wide[:, :, :head] = q_raw[...].astype(jnp.float32)
    plain = q_wide[...].reshape(batch * heads, LANES)
    turned = plain
    turns = LANES // math.gcd(head, LANES)
    for row in range(1, turns):
        take = lax.rem(lax.broadcasted_iota(jnp.int32, plain.shape, 0), turns) == row
        turned = jnp.where(take, pltpu.roll(plain, row * head % LANES, 1), turned)
    q_wide[...] = turned.reshape(batch, heads, LANES)

    row = lax.broadcasted_iota(jnp.int32, (ROWS, LANES), 0)
    lane = lax.broadcasted_iota(jnp.int32, (ROWS, LANES), 1)
    inside = []
    for block in range(span // LANES):
        at = lane + block * LANES - row * head
        inside.append((at >= 0) & (at < head))

    def weigh(j, g):
        phase, step = where(j)
        slot = j & (SLOTS - 1)
        at = slice(g * ROWS, (g + 1) * ROWS)
        query = q_wide[peer(step) * own + g // groups, pl.ds(phase * some + g % groups * ROWS, ROWS), :]
        query = jnp.concatenate([jnp.where(i, query, 0.0) for i in inside], 1).astype(jnp.bfloat16)
        key = keys[slot, g // groups, pl.ds(g % groups * span, span), :]
        scores = jnp.dot(query, key, preferred_element_type=jnp.float32) * head**-0.5
        high = jnp.max(scores, -1, keepdims=True)
        drawn = jnp.exp(scores - high)
        total = jnp.sum(drawn, -1, keepdims=True)
        weights[at, :] = drawn.astype(jnp.bfloat16)
        parts[phase * n + step, at, :] = jnp.where(lane == head, total, jnp.broadcast_to(high, lane.shape))

    def gather(j, g, drawn):
        values_g = values[j & (SLOTS - 1), g // groups, pl.ds(g % groups * span, span), :]
        sums = lax.dot_general(drawn, values_g, (((1,), (1,)), ((), ())), preferred_element_type=jnp.float32)
        mine = sums[:, :LANES]
        for block in range(1, span // LANES):
            mine = jnp.where(inside[block], sums[:, block * LANES : (block + 1) * LANES], mine)
        seen[g * ROWS : (g + 1) * ROWS, :] = mine

    def finish(j, mine):
        phase, step = where(j)
        for g in range(own * groups):
            at = slice(g * ROWS, (g + 1) * ROWS)
            turned = mine[at]
            for _ in range((LANES - head) // TURN):
                turned = pltpu.roll(turned, 0, 1, stride=TURN, stride_axis=0)
            parts[phase * n + step, at, :head] = turned[:, :head]

    def attend(j, behind, ahead):
        drawn = [weights[g * ROWS : (g + 1) * ROWS, :] for g in range(own * groups)]
        if behind:
            finish(j - 1, seen[...])
        for g in range(own * groups):
            if ahead:
                weigh(j + 1, g)
            gather(j, g, drawn[g])

    def send(phase, step):
        index = phase * n + step
        return pltpu.make_async_remote_copy(
            src_ref=parts.at[index],
            dst_ref=others.at[index],
            send_sem=send_sem.at[index],
            recv_sem=recv_sem.at[index],
            device_id={"sp": peer(step)},
            device_id_type=MESH,
        )

    def refill(j):
        @pl.when(j + 1 + SLOTS < units + PHASES)
        def _():
            fetch_k(j + 1 + SLOTS).start()

        @pl.when(j + SLOTS < units + PHASES)
        def _():
            fetch_v(j + SLOTS).start()

    def work(j, _):
        fetch_k(j + 1).wait()
        fetch_v(j).wait()
        attend(j, True, True)
        send(*where(j - 1)).start()
        refill(j)
        return 0

    def give(phase, step):
        index = phase * n + step
        return pltpu.make_async_remote_copy(
            src_ref=done.at[phase],
            dst_ref=out_ref.at[pl.ds(me * own, own), pl.ds(phase * some, some)],
            send_sem=out_send.at[index],
            recv_sem=out_recv.at[index],
            device_id={"sp": peer(step)},
            device_id_type=MESH,
        )

    def keep(phase):
        return pltpu.make_async_copy(done.at[phase], out_ref.at[pl.ds(me * own, own), pl.ds(phase * some, some)], own_sem.at[phase])

    def far(step):
        side = math.isqrt(n)
        return sum(min(d, side - d) for d in (step // side, step % side))

    def settle(phase):
        steps = [0] + [step for step in range(n - 1, 0, -1)]
        sums, top = None, None
        for some_steps in (steps[:-LATE], steps[-LATE:]):
            runs = []
            for step in some_steps:
                if step:
                    send(phase, step).wait_recv()
                runs.append((others if step else parts)[phase * n + step])
            highs = [jnp.broadcast_to(run[:, head + 1 : head + 2], run.shape) for run in runs]
            if sums is not None:
                runs.append(sums)
                highs.append(top)
            top = functools.reduce(jnp.maximum, highs)
            sums = sum(run * jnp.exp(high - top) for run, high in zip(runs, highs))
        result = sums[:, :head] / sums[:, head : head + 1]
        done[phase] = result.astype(jnp.bfloat16).reshape(own, some, head)
        for step in sorted(range(1, n), key=far, reverse=True):
            give(phase, step).start()
        keep(phase).start()

    fetch_k(0).wait()
    for g in range(own * groups):
        weigh(0, g)
    fetch_k(SLOTS).start()
    pl.semaphore_wait(barrier, n - 1)
    fetch_k(1).wait()
    fetch_v(0).wait()
    attend(0, False, True)
    refill(0)
    lax.fori_loop(1, units, work, 0)
    finish(units - 1, seen[...])
    send(*where(units - 1)).start()
    for phase in range(PHASES):
        j = units + phase
        ahead = phase + 1 < PHASES
        if ahead:
            fetch_k(j + 1).wait()
        fetch_v(j).wait()
        attend(j, False, ahead)
        finish(j, seen[...])
        settle(phase)

    def drain(index, _):
        phase, step = index // (n - 1), lax.rem(index, n - 1) + 1
        send(phase, step).wait_send()
        give(phase, step).wait()
        return 0

    lax.fori_loop(0, units, drain, 0)
    for phase in range(PHASES):
        keep(phase).wait()


def solution(mesh):
    n = mesh.shape["sp"]

    def step(q, k, v):
        batch, tokens, heads, head = k.shape
        own = batch // n
        some = heads // PHASES
        rows = own * some
        flat = lambda x: x.transpose(0, 2, 3, 1).reshape(batch, heads * head, tokens)
        return pl.pallas_call(
            functools.partial(kernel, n),
            out_shape=jax.ShapeDtypeStruct(q.shape, jnp.bfloat16),
            in_specs=[pl.BlockSpec(memory_space=pl.ANY)] * 3,
            out_specs=pl.BlockSpec(memory_space=pl.ANY),
            scratch_shapes=[
                pltpu.VMEM(q.shape, jnp.bfloat16),
                pltpu.VMEM((batch, heads, LANES), jnp.float32),
                pltpu.VMEM((SLOTS, own, some * head, tokens), jnp.bfloat16),
                pltpu.VMEM((SLOTS, own, some * head, tokens), jnp.bfloat16),
                pltpu.VMEM((rows, tokens), jnp.bfloat16),
                pltpu.VMEM((rows, LANES), jnp.float32),
                pltpu.VMEM((PHASES * n, rows, LANES), jnp.float32),
                pltpu.VMEM((PHASES * n, rows, LANES), jnp.float32),
                pltpu.VMEM((PHASES, own, some, head), jnp.bfloat16),
                pltpu.SemaphoreType.DMA,
                pltpu.SemaphoreType.DMA((SLOTS,)),
                pltpu.SemaphoreType.DMA((SLOTS,)),
                pltpu.SemaphoreType.DMA((PHASES * n,)),
                pltpu.SemaphoreType.DMA((PHASES * n,)),
                pltpu.SemaphoreType.DMA((PHASES * n,)),
                pltpu.SemaphoreType.DMA((PHASES * n,)),
                pltpu.SemaphoreType.DMA((PHASES,)),
            ],
            compiler_params=pltpu.CompilerParams(collective_id=0, has_side_effects=True, vmem_limit_bytes=48 * 2**20),
        )(q, flat(k), flat(v))

    return jax.shard_map(
        step,
        mesh=mesh,
        in_specs=(P("dp", None, None), P("dp", "sp", None, None), P("dp", "sp", None, None)),
        out_specs=P("dp", None, None),
        check_vma=False,
    )
```

time: 154 us -> 44.9 us (0.29)
  waiting for transfers between devices: 69.3 us -> 0 us
  Pallas kernels: 0 us -> 42.9 us
  matrix products: 37.7 us -> 0 us
  local copies, waits for them, and re-layouts: 19.1 us -> 1.65 us
  other arithmetic: 14.1 us -> 0 us
  between operations: 13.5 us -> 0.01 us
    all_gather x1 -> x0, waiting for transfers between devices: 69.3 us -> none  [step(): return together(lax.all_gather(part_of(q, k, v), 'sp')).reshape(q.shape)]
    pallas_call x0 -> x1, Pallas kernels: none -> 42.9 us  [step(): pl.pallas_call(functools.partial(kernel, n), out_shape=jax.ShapeDtypeStru...]
    dot_general x2 -> x0, matrix products: 37.7 us -> none  [einsum(): return jnp.einsum(form, a.astype(jnp.float32), b.astype(jnp.float32))]
    all_gather x1 -> x0, local copies, waits for them, and re-layouts: 17 us -> none  [step(): return together(lax.all_gather(part_of(q, k, v), 'sp')).reshape(q.shape)]
    reduce_sum x2 -> x0, other arithmetic: 11.1 us -> none  [the longest x1 10 us: together(): jnp.sum(seen * scale, 0) / jnp.sum(total * scale, 0)]
    unnamed x0 -> x3, local copies, waits for them, and re-layouts: none -> 1.65 us
  transfers between devices with their start and end apart: 1 -> 0, of which waited for: 1 -> 0; matrix products, arithmetic and copies ran while one was open for 0% -> 0% of each run, Pallas kernels for 0% -> 0%
where the time goes in v3:
time: 44.9 us; the launch traced here: 44.6 us
  Pallas kernels  42.9 us (96%)
  local copies, waits for them, and re-layouts  1.65 us (4%)
    pallas_call x1, Pallas kernels, step(): pl.pallas_call(functools.partial(kernel, n), out_shape=jax.ShapeDtypeStru...  42.9 us
    unnamed x3, local copies, waits for them, and re-layouts  1.65 us

profile of v3, /device:TPU:97, one launch (start us, length us, event | category | flops | bytes accessed | tf_op | source)
XLA Modules:
  0.0 44.6 jit_solution(16158837797189933728)
XLA Ops:
  0.0 0.0 copy-start
  0.0 0.9 %copy-done = bf16[32,32,96]{2,1,0:T(8,128)(2,1)S(1)} copy-done((bf16[32,32,96]{2,1,0:T(8,128)(2,1)S(1)}, bf16[32,32,96]{2,1,0:T(8,128)(2,1)}, u32[]{:S(2)}) %copy-start) | copy-done | bytes 196632
  1.0 42.9 %shard_map.37 = bf16[32,32,96]{2,1,0:T(8,128)(2,1)S(1)} custom-call(bf16[32,32,96]{2,1,0:T(8,128)(2,1)S(1)} %copy-done, bf16[32,3072,256]{2,1,0:T(8,128)(2,1)} %bitcast.6, bf16[32,3072,256]{2,1,0:T(8,128)(2,1)} %bitcast.7), custom_call_target="tpu_custom_call" | custom-call | tf_op jit(solution)/shard_map/pallas_call | solution.py:232
  43.9 0.7 %copy.5 = bf16[32,32,96]{2,1,0:T(8,128)(2,1)} copy(bf16[32,32,96]{2,1,0:T(8,128)(2,1)S(1)} %shard_map.37) | data formatting | bytes 393216
Async XLA Ops:
  0.0 0.9 %copy-start = (bf16[32,32,96]{2,1,0:T(8,128)(2,1)S(1)}, bf16[32,32,96]{2,1,0:T(8,128)(2,1)}, u32[]{:S(2)}) copy-start(bf16[32,32,96]{2,1,0:T(8,128)(2,1)} %q_hbm.1) | copy-start | bytes 589828

commit v4 on v3

--- a/solution.py
+++ b/solution.py
@@ -11,9 +11,8 @@
 MESH = pl.DeviceIdType.MESH
 LANES = 128
 ROWS = 8
-TURN = 16
 PHASES = 2
-LATE = 4
+LATE = 3
 SLOTS = 4
 
 
@@ -52,10 +51,8 @@
 
     q_copy = pltpu.make_async_copy(q_hbm, q_raw, q_sem)
     q_copy.start()
-    for j in range(SLOTS):
-        fetch_k(j).start()
-        fetch_v(j).start()
-
+    fetch_k(0).start()
+    fetch_v(0).start()
     barrier = pltpu.get_barrier_semaphore()
 
     def greet(step, _):
@@ -63,14 +60,17 @@
         return 0
 
     lax.fori_loop(1, n, greet, 0)
+    for j in range(1, SLOTS):
+        fetch_k(j).start()
+        fetch_v(j).start()
     q_copy.wait()
     q_wide[:, :, :head] = q_raw[...].astype(jnp.float32)
     plain = q_wide[...].reshape(batch * heads, LANES)
     turned = plain
     turns = LANES // math.gcd(head, LANES)
-    for row in range(1, turns):
-        take = lax.rem(lax.broadcasted_iota(jnp.int32, plain.shape, 0), turns) == row
-        turned = jnp.where(take, pltpu.roll(plain, row * head % LANES, 1), turned)
+    for h in range(1, turns):
+        take = lax.rem(lax.broadcasted_iota(jnp.int32, plain.shape, 0), turns) == h
+        turned = jnp.where(take, pltpu.roll(plain, h * head % LANES, 1), turned)
     q_wide[...] = turned.reshape(batch, heads, LANES)
 
     row = lax.broadcasted_iota(jnp.int32, (ROWS, LANES), 0)
@@ -107,8 +107,8 @@
         for g in range(own * groups):
             at = slice(g * ROWS, (g + 1) * ROWS)
             turned = mine[at]
-            for _ in range((LANES - head) // TURN):
-                turned = pltpu.roll(turned, 0, 1, stride=TURN, stride_axis=0)
+            for h in range(1, turns):
+                turned = jnp.where(row % turns == h, pltpu.roll(mine[at], -h * head % LANES, 1), turned)
             parts[phase * n + step, at, :head] = turned[:, :head]
 
     def attend(j, behind, ahead):
@@ -132,13 +132,13 @@
         )
 
     def refill(j):
+        @pl.when(j + SLOTS < units + PHASES)
+        def _():
+            fetch_v(j + SLOTS).start()
+
         @pl.when(j + 1 + SLOTS < units + PHASES)
         def _():
             fetch_k(j + 1 + SLOTS).start()
-
-        @pl.when(j + SLOTS < units + PHASES)
-        def _():
-            fetch_v(j + SLOTS).start()
 
     def work(j, _):
         fetch_k(j + 1).wait()
@@ -166,24 +166,24 @@
         side = math.isqrt(n)
         return sum(min(d, side - d) for d in (step // side, step % side))
 
-    def settle(phase):
-        steps = [0] + [step for step in range(n - 1, 0, -1)]
-        sums, top = None, None
-        for some_steps in (steps[:-LATE], steps[-LATE:]):
-            runs = []
-            for step in some_steps:
-                if step:
-                    send(phase, step).wait_recv()
-                runs.append((others if step else parts)[phase * n + step])
-            highs = [jnp.broadcast_to(run[:, head + 1 : head + 2], run.shape) for run in runs]
-            if sums is not None:
-                runs.append(sums)
-                highs.append(top)
-            top = functools.reduce(jnp.maximum, highs)
-            sums = sum(run * jnp.exp(high - top) for run, high in zip(runs, highs))
-        result = sums[:, :head] / sums[:, head : head + 1]
+    def arrive(phase, steps):
+        for step in steps:
+            send(phase, step).wait_recv()
+
+    def merge(phase, steps, before):
+        runs = [(others if step else parts)[phase * n + step] for step in steps]
+        highs = [jnp.broadcast_to(run[:, head + 1 : head + 2], run.shape) for run in runs]
+        totals = [jnp.broadcast_to(run[:, head : head + 1], run.shape) for run in runs]
+        if before is not None:
+            runs, highs, totals = runs + [before[0]], highs + [before[1]], totals + [before[2]]
+        high = functools.reduce(jnp.maximum, highs)
+        scales = [jnp.exp(h - high) for h in highs]
+        return sum(r * x for r, x in zip(runs, scales)), high, sum(t * x for t, x in zip(totals, scales))
+
+    def share(phase, merged):
+        result = merged[0][:, :head] / merged[2][:, :head]
         done[phase] = result.astype(jnp.bfloat16).reshape(own, some, head)
-        for step in sorted(range(1, n), key=far, reverse=True):
+        for step in reversed(by_distance):
             give(phase, step).start()
         keep(phase).start()
 
@@ -191,33 +191,49 @@
     for g in range(own * groups):
         weigh(0, g)
     fetch_k(SLOTS).start()
-    pl.semaphore_wait(barrier, n - 1)
     fetch_k(1).wait()
     fetch_v(0).wait()
     attend(0, False, True)
     refill(0)
-    lax.fori_loop(1, units, work, 0)
-    finish(units - 1, seen[...])
-    send(*where(units - 1)).start()
+    pl.semaphore_wait(barrier, n - 1)
+    lax.fori_loop(1, units - 1, work, 0)
+
+    by_distance = sorted(range(1, n), key=far)
+    early = list(range(n - 1, LATE, -1))
+    late = list(range(LATE, 0, -1))
+    j = units - 1
+    fetch_v(j).wait()
+    attend(j, True, False)
+    send(*where(j - 1)).start()
+    finish(j, seen[...])
+    send(*where(j)).start()
+    fetch_k(units).wait()
+    for g in range(own * groups):
+        weigh(units, g)
     for phase in range(PHASES):
         j = units + phase
         ahead = phase + 1 < PHASES
         if ahead:
             fetch_k(j + 1).wait()
+        if phase:
+            arrive(phase - 1, early + late)
         fetch_v(j).wait()
         attend(j, False, ahead)
+        if phase:
+            share(phase - 1, merge(phase - 1, [0] + early + late, None))
         finish(j, seen[...])
-        settle(phase)
-
-    def drain(index, _):
-        phase, step = index // (n - 1), lax.rem(index, n - 1) + 1
-        send(phase, step).wait_send()
-        give(phase, step).wait()
-        return 0
-
-    lax.fori_loop(0, units, drain, 0)
+    arrive(phase, early)
+    merged = merge(phase, [0] + early, None)
+    arrive(phase, late)
+    share(phase, merge(phase, late, merged))
+
+    for phase in range(PHASES):
+        for step in range(1, n):
+            send(phase, step).wait_send()
     for phase in range(PHASES):
         keep(phase).wait()
+        for step in by_distance:
+            give(phase, step).wait()
 
 
 def solution(mesh):
@@ -254,7 +270,7 @@
                 pltpu.SemaphoreType.DMA((PHASES,)),
             ],
             compiler_params=pltpu.CompilerParams(collective_id=0, has_side_effects=True, vmem_limit_bytes=48 * 2**20),
-        )(q, flat(k), flat(v))
+        )(pltpu.with_memory_space_constraint(q, pltpu.HBM), flat(k), flat(v))
 
     return jax.shard_map(
         step,

time: 44.9 us -> 43.6 us (0.971)
  local copies, waits for them, and re-layouts: 1.65 us -> 0.71 us
    unnamed x3 -> x1, local copies, waits for them, and re-layouts: 1.65 us -> 0.71 us
where the time goes in v4:
time: 43.6 us; the launch traced here: 43.5 us
  Pallas kernels  42.8 us (98%)
  local copies, waits for them, and re-layouts  0.71 us (2%)
    pallas_call x1, Pallas kernels, step(): pl.pallas_call(functools.partial(kernel, n), out_shape=jax.ShapeDtypeStru...  42.8 us

profile of v4, /device:TPU:97, one launch (start us, length us, event | category | flops | bytes accessed | tf_op | source)
XLA Modules:
  0.0 43.5 jit_solution(10988798841675649109)
XLA Ops:
  0.0 42.8 %shard_map.37 = bf16[32,32,96]{2,1,0:T(8,128)(2,1)S(1)} custom-call(bf16[32,32,96]{2,1,0:T(8,128)(2,1)} %q_hbm.1, bf16[32,3072,256]{2,1,0:T(8,128)(2,1)} %bitcast.6, bf16[32,3072,256]{2,1,0:T(8,128)(2,1)} %bitcast.7), custom_call_target="tpu_custom_call" | custom-call | tf_op jit(solution)/shard_map/pallas_call | solution.py:248
  42.8 0.7 %copy.5 = bf16[32,32,96]{2,1,0:T(8,128)(2,1)} copy(bf16[32,32,96]{2,1,0:T(8,128)(2,1)S(1)} %shard_map.37) | data formatting | bytes 393216

commit v5 on v4

--- a/solution.py
+++ b/solution.py
@@ -13,7 +13,7 @@
 ROWS = 8
 PHASES = 2
 LATE = 3
-SLOTS = 4
+SLOTS = 8
 
 
 def kernel(

time: 43.6 us -> 43.6 us (level)
  no operation moved by 1% of the time
where the time goes in v5:
time: 43.6 us; the launch traced here: 43.5 us
  Pallas kernels  42.8 us (98%)
  local copies, waits for them, and re-layouts  0.71 us (2%)
    pallas_call x1, Pallas kernels, step(): pl.pallas_call(functools.partial(kernel, n), out_shape=jax.ShapeDtypeStru...  42.8 us

profile of v5, /device:TPU:97, one launch (start us, length us, event | category | flops | bytes accessed | tf_op | source)
XLA Modules:
  0.0 43.5 jit_solution(17074495804732731119)
XLA Ops:
  0.0 42.8 %shard_map.37 = bf16[32,32,96]{2,1,0:T(8,128)(2,1)S(1)} custom-call(bf16[32,32,96]{2,1,0:T(8,128)(2,1)} %q_hbm.1, bf16[32,3072,256]{2,1,0:T(8,128)(2,1)} %bitcast.6, bf16[32,3072,256]{2,1,0:T(8,128)(2,1)} %bitcast.7), custom_call_target="tpu_custom_call" | custom-call | tf_op jit(solution)/shard_map/pallas_call | solution.py:248
  42.8 0.7 %copy.5 = bf16[32,32,96]{2,1,0:T(8,128)(2,1)} copy(bf16[32,32,96]{2,1,0:T(8,128)(2,1)S(1)} %shard_map.37) | data formatting | bytes 393216
